TPU v7x, 32 devices: a whole 2x2x4 slice. The times are simulated.
32 devices in a mesh: real: 2 (over y), col: 8 (over z, x), row: 2 (over core).
Axes of the slice: x: 2, y: 2, z: 4, core: 2. Of those that a mesh axis runs over, the one named last changes fastest.
Arguments:
- theta: bfloat16 [512, 16384], P(('real', 'row'), 'col'), parts along dimension 0, may hold values from -6 to 6
- signs: int32 [32768], P(('real', 'col')), parts along dimension 0, may hold values from -1 to 1, as said below
- kept: int32 [1024], replicated, may hold values from 0 to 16383, as said below
Outputs:
- gram: float32 [4, 8, 16, 256], P(('real', 'row'), 'col'), parts along dimension 0
There are 2 independent parts, one for each index of `real`. A program takes and returns all parts, laid end to end along the dimension named above; an argument that names none is the same for every part. Nothing has to cross between parts.
Inputs may be any that keep to these rules, and one draw needn't show every extreme that they name: `signs`: each entry is -1 or 1. `kept`: 1024 distinct column indices.
All inputs are finite; a program needn't handle non-finite values.
Results may differ from a plain program's by a relative error of at most 0.0036.
Values may be sent and summed in bfloat16 or wider, within the bound.
No kernel may reach another device: no remote copies, remote signals or barrier semaphores. Data moves between devices by JAX's collectives and lax.ppermute only.
A program may use at most 64 MiB of HBM per device.

v0:
```python
import jax
import jax.numpy as jnp
from jax import lax
from jax.sharding import PartitionSpec as P

SIDE = 128
KEEP = 1024


def hadamard(order, dtype):
    indices = jnp.arange(order, dtype=jnp.int32)
    common = indices[:, None] & indices[None, :]
    parity = jnp.zeros((order, order), jnp.int32)
    for position in range(order.bit_length() - 1):
        parity = parity ^ common >> position & 1
    return (1 - 2 * parity).astype(dtype)


def against(left, right):
    return jnp.dot(left, right.T, preferred_element_type=jnp.float32)


def two_factor(spread):
    height = spread.shape[0]
    flat = spread.reshape(height * SIDE, SIDE)
    inner = jnp.dot(flat, hadamard(SIDE, jnp.bfloat16), preferred_element_type=jnp.float32).reshape(
        height, SIDE, SIDE
    )
    outer = jnp.einsum(
        "rak,aj->rjk", inner, hadamard(SIDE, jnp.float32), precision=lax.Precision.HIGHEST
    )
    return outer.reshape(height, SIDE * SIDE)


def per_device(theta, signs, kept):
    scaled = theta * signs.astype(jnp.bfloat16)[None, :]
    spread = lax.all_to_all(scaled, "col", split_axis=0, concat_axis=1, tiled=True)
    transformed = two_factor(spread) / SIDE
    sketch = jnp.take(transformed, kept, axis=1).astype(jnp.bfloat16)
    own_rows = sketch.shape[0]
    half_rows = lax.all_gather(sketch, "col", axis=0, tiled=True)
    gram = against(sketch, lax.all_gather(half_rows, "row", axis=0, tiled=True))
    return (gram / KEEP).reshape(1, 1, own_rows, gram.shape[1])


def solution(mesh):
    return jax.shard_map(
        per_device,
        mesh=mesh,
        in_specs=(P(("real", "row"), "col"), P(("real", "col")), P()),
        out_specs=P(("real", "row"), "col", None, None),
        check_vma=False,
    )
```

profile of v0, /device:TPU:0, one launch (start us, length us, event | category | flops | bytes accessed | tf_op | source)
XLA Modules:
  0.0 69.4 jit_solution(3105334876577274971)
XLA Ops:
  0.0 0.7 %convert_element_type.13 = bf16[2048]{0:T(1024)(128)(2,1)S(1)} convert(s32[2048]{0:T(1024)} %param.4) | non-fusion elementwise | flops 2048 | bytes 12288 | tf_op jit(solution)/shard_map/convert_element_type | solution.py:36
  0.7 1.9 %broadcast_multiply_fusion = bf16[128,2048]{1,0:T(8,128)(2,1)} fusion(bf16[128,2048]{1,0:T(8,128)(2,1)} %param.3, bf16[2048]{0:T(1024)(128)(2,1)S(1)} %convert_element_type.13), kind=kLoop, calls=%fused_computation.6 | loop fusion | flops 262144 | bytes 1052672 | tf_op jit(solution)/shard_map/mul | solution.py:36
  2.6 7.3 %all-to-all-start = ((bf16[8,16,2048]{2,1,0:T(8,128)(2,1)}), bf16[8,16,2048]{2,1,0:T(8,128)(2,1)S(1)}, u32[]{:S(2)}, u32[]{:S(2)}) async-start(bf16[8,16,2048]{2,1,0:T(8,128)(2,1)} %bitcast.1), calls=%async_computation | async-start | bytes 1048576 | tf_op jit(solution)/shard_map/all_to_all | solution.py:37
  9.8 0.7 compare_and_fusion
  10.5 0.7 fusion.7
  11.2 13.1 %all-to-all-done = bf16[8,16,2048]{2,1,0:T(8,128)(2,1)S(1)} async-done(((bf16[8,16,2048]{2,1,0:T(8,128)(2,1)}), bf16[8,16,2048]{2,1,0:T(8,128)(2,1)S(1)}, u32[]{:S(2)}, u32[]{:S(2)}) %all-to-all-start) | async-done | bytes 524320 | tf_op jit(solution)/shard_map/all_to_all | solution.py:37
  24.3 0.3 copy.7
  24.6 0.2 dot_general.11
  24.9 0.3 fusion.4
  25.2 1.1 %fusion = bf16[16,128,128]{2,1,0:T(8,128)(2,1)S(1)} fusion(f32[16,128,128]{2,1,0:T(8,128)S(1)} %fusion.4), kind=kOutput, calls=%fused_computation.2 | convolution fusion | flops 403570688 | bytes 1572864 | tf_op jit(solution)/shard_map/rak,aj->rjk/dot_general | solution.py:29
  26.3 3.2 %copy.13 = bf16[16,128,128]{0,2,1:T(8,128)(2,1)} copy(bf16[16,128,128]{2,1,0:T(8,128)(2,1)S(1)} %fusion) | data formatting | bytes 1048576 | tf_op jit(solution)/shard_map/div | solution.py:38
  29.5 5.6 %gather_fusion = bf16[1024,16]{1,0:T(8,128)(2,1)S(1)} fusion(bf16[16,16384]{0,1:T(8,128)(2,1)} %bitcast.18, s32[1024]{0:T(1024)S(1)} %fusion.7), kind=kCustom, calls=%fused_computation | custom fusion | bytes 69632 | tf_op jit(solution)/shard_map/jit(_take)/gather | solution.py:39
  35.1 0.2 fusion.22
  35.3 0.1 copy.10
  35.4 30.7 %all_gather.6 = bf16[128,1024]{1,0:T(8,128)(2,1)S(1)} all-gather(bf16[16,1024]{1,0:T(8,128)(2,1)S(1)} %copy.10), channel_id=1, replica_groups=mesh['real'=2,'col'=8,'row'=2] {'col'}, dimensions={0}, use_global_device_ids=true | all-gather | bytes 294912 | tf_op jit(solution)/shard_map/all_gather | solution.py:41
  66.1 2.2 %all_gather.7 = bf16[256,1024]{1,0:T(8,128)(2,1)S(1)} all-gather(bf16[128,1024]{1,0:T(8,128)(2,1)S(1)} %all_gather.6), channel_id=1, replica_groups=mesh['real'=2,'col'=8,'row'=2] {'row'}, dimensions={0}, use_global_device_ids=true | all-gather | bytes 786432 | tf_op jit(solution)/shard_map/all_gather | solution.py:42
  68.3 1.1 %fusion.1 = f32[1,1,16,256]{3,2,1,0:T(8,128)} fusion(bf16[256,1024]{1,0:T(8,128)(2,1)S(1)} %all_gather.7, bf16[1024,16]{1,0:T(8,128)(2,1)S(1)} %gather_fusion, pred[1024]{0:T(1024)(128)(4,1)S(1)} %compare_and_fusion), kind=kOutput, calls=%fused_computation.4 | convolution fusion | flops 8409088 | bytes 574464 | tf_op jit(solution)/shard_map/dot_general | solution.py:20
Async XLA Ops:
  2.6 21.8 %all-to-all-start = ((bf16[8,16,2048]{2,1,0:T(8,128)(2,1)}), bf16[8,16,2048]{2,1,0:T(8,128)(2,1)S(1)}, u32[]{:S(2)}, u32[]{:S(2)}) async-start(bf16[8,16,2048]{2,1,0:T(8,128)(2,1)} %bitcast.1), calls=%async_computation | async-start | bytes 1048576 | tf_op jit(solution)/shard_map/all_to_all | solution.py:37
where the time goes:
time: 69.8 us; the launch traced here: 69.4 us
  blocking collectives  32.9 us (47%)
  waiting for transfers between devices  13.1 us (19%)
  local copies, waits for them, and re-layouts  9.42 us (13%)
  starting transfers between devices  7.28 us (10%)
  other arithmetic  4.14 us (6%)
  matrix products  2.5 us (4%)
    all_gather x1, blocking collectives, per_device(): half_rows = lax.all_gather(sketch, 'col', axis=0, tiled=True)  30.7 us
    all_to_all x1, waiting for transfers between devices, per_device(): lax.all_to_all(scaled, 'col', split_axis=0, concat_axis=1, tiled=True)  13.1 us
    all_to_all x1, starting transfers between devices, per_device(): lax.all_to_all(scaled, 'col', split_axis=0, concat_axis=1, tiled=True)  7.28 us
    gather x1, local copies, waits for them, and re-layouts, per_device(): sketch = jnp.take(transformed, kept, axis=1).astype(jnp.bfloat16)  5.6 us
    div x1, local copies, waits for them, and re-layouts, per_device(): transformed = two_factor(spread) / SIDE  3.17 us
    all_gather x1, blocking collectives, per_device(): gram = against(sketch, lax.all_gather(half_rows, 'row', axis=0, tiled=True))  2.17 us
    mul x1, other arithmetic, per_device(): scaled = theta * signs.astype(jnp.bfloat16)[None, :]  1.86 us
  transfers between devices with their start and end apart: 1, of which 1 were waited for; matrix products, arithmetic and copies ran while one was open for 2% of the time, Pallas kernels for 0%

commit v1 on v0

v1 whole, which is shorter than its diff:
```python
import functools

import jax
import jax.numpy as jnp
from jax import lax
from jax.experimental import pallas as pl
from jax.experimental.pallas import tpu as pltpu
from jax.sharding import PartitionSpec as P

SIDE = 128


def sign_of(bits, shift=4):
    while shift:
        bits = bits ^ bits >> shift
        shift //= 2
    return (1 - 2 * (bits & 1)).astype(jnp.float32).astype(jnp.bfloat16)


def partial_kernel(theta_ref, signs_ref, kept_ref, out_ref, table_ref, *, by_block):
    rows, local = theta_ref.shape
    keep = kept_ref.shape[1]
    groups = local // SIDE
    first = lax.axis_index("col") * groups
    kept = kept_ref[...]
    low = sign_of(lax.broadcasted_iota(jnp.int32, (SIDE, keep), 0) & kept)
    for group in range(groups):
        high = sign_of((kept >> 7) & (first + group))
        table_ref[group * SIDE : (group + 1) * SIDE, :] = low * high
    scaled = theta_ref[...] * signs_ref[...].astype(jnp.float32).astype(jnp.bfloat16)
    part = jnp.dot(scaled, table_ref[...], preferred_element_type=jnp.float32)
    if by_block:
        width = out_ref.shape[2]
        for block in range(out_ref.shape[0]):
            out_ref[block] = part[:, block * width : (block + 1) * width].astype(jnp.bfloat16)
    else:
        out_ref[...] = part.T.astype(jnp.bfloat16)


def partial_sketch(theta, signs, kept, parts):
    rows, local = theta.shape
    keep = kept.shape[0]
    width = keep // parts
    by_block = width % SIDE == 0
    shape = (parts, rows, width) if by_block else (keep, rows)
    out = pl.pallas_call(
        functools.partial(partial_kernel, by_block=by_block),
        out_shape=jax.ShapeDtypeStruct(shape, jnp.bfloat16),
        in_specs=[pl.BlockSpec(memory_space=pltpu.VMEM)] * 3,
        out_specs=pl.BlockSpec(memory_space=pltpu.VMEM),
        scratch_shapes=[pltpu.VMEM((local, keep), jnp.bfloat16)],
        name="partial_sketch",
    )(theta, signs.reshape(1, local), kept.reshape(1, keep))
    return out if by_block else out.reshape(parts, width, rows).swapaxes(1, 2)


def per_device(parts, halves, length, theta, signs, kept):
    keep = kept.shape[0]
    rows = theta.shape[0]
    part = partial_sketch(theta, signs, kept, parts)
    met = lax.all_to_all(part, "col", split_axis=0, concat_axis=0, tiled=True)
    sketch = (met.astype(jnp.float32).sum(0) / SIDE).astype(jnp.bfloat16)
    other = lax.ppermute(sketch, "row", [(i, (i + 1) % halves) for i in range(halves)])
    own = lax.axis_index("row") == 0
    both = jnp.concatenate([jnp.where(own, sketch, other), jnp.where(own, other, sketch)], axis=0)
    gram = jnp.dot(sketch, both.T, preferred_element_type=jnp.float32).astype(jnp.bfloat16)
    met = lax.all_to_all(gram.reshape(parts, rows // parts, -1), "col", split_axis=0, concat_axis=0, tiled=True)
    return (met.astype(jnp.float32).sum(0) / keep)[None, None]


def solution(mesh):
    parts, halves = mesh.shape["col"], mesh.shape["row"]
    return jax.shard_map(
        functools.partial(per_device, parts, halves, None),
        mesh=mesh,
        in_specs=(P(("real", "row"), "col"), P(("real", "col")), P()),
        out_specs=P(("real", "row"), "col", None, None),
        check_vma=False,
    )
```

time: 69.8 us -> 31.5 us (0.45)
  waiting for transfers between devices: 13.1 us -> 1.19 us
  local copies, waits for them, and re-layouts: 9.42 us -> 0 us
  starting transfers between devices: 7.28 us -> 0.07 us
  blocking collectives: 32.9 us -> 26.5 us
  other arithmetic: 4.14 us -> 0.68 us
  Pallas kernels: 0 us -> 2.66 us
  matrix products: 2.5 us -> 0.16 us
    all_gather x2 -> x0, blocking collectives: 32.9 us -> none  [the longest x1 30.7 us: per_device(): half_rows = lax.all_gather(sketch, 'col', axis=0, tiled=True)]
    all_to_all x0 -> x2, blocking collectives: none -> 26.5 us  [the longest x1 16.2 us: per_device(): met = lax.all_to_all(part, 'col', split_axis=0, concat_axis=0, tiled=True)]
    all_to_all x1 -> x0, waiting for transfers between devices: 13.1 us -> none  [per_device(): lax.all_to_all(scaled, 'col', split_axis=0, concat_axis=1, tiled=True)]
    all_to_all x1 -> x0, starting transfers between devices: 7.28 us -> none  [per_device(): lax.all_to_all(scaled, 'col', split_axis=0, concat_axis=1, tiled=True)]
    gather x1 -> x0, local copies, waits for them, and re-layouts: 5.6 us -> none  [per_device(): sketch = jnp.take(transformed, kept, axis=1).astype(jnp.bfloat16)]
    div x1 -> x0, local copies, waits for them, and re-layouts: 3.17 us -> none  [per_device(): transformed = two_factor(spread) / SIDE]
    pallas_call x0 -> x1, Pallas kernels: none -> 2.66 us  [partial_sketch(): pl.pallas_call(functools.partial(partial_kernel, by_block=by_block), out_...]
    dot_general x3 -> x1, matrix products: 2.5 us -> 0.16 us  [per_device(): jnp.dot(sketch, both.T, preferred_element_type=jnp.float32)]
  transfers between devices with their start and end apart: 1 -> 1, of which waited for: 1 -> 1; matrix products, arithmetic and copies ran while one was open for 2% -> 0% of each run, Pallas kernels for 0% -> 0%
where the time goes in v1:
time: 31.5 us; the launch traced here: 31.3 us
  blocking collectives  26.5 us (84%)
  Pallas kernels  2.66 us (8%)
  waiting for transfers between devices  1.19 us (4%)
  other arithmetic  0.68 us (2%)
    all_to_all x1, blocking collectives, per_device(): met = lax.all_to_all(part, 'col', split_axis=0, concat_axis=0, tiled=True)  16.2 us
    all_to_all x1, blocking collectives, per_device(): lax.all_to_all(gram.reshape(parts, rows // parts, -1), 'col', split_axis=...  10.3 us
    pallas_call x1, Pallas kernels, partial_sketch(): pl.pallas_call(functools.partial(partial_kernel, by_block=by_block), out_...  2.66 us
    ppermute x1, waiting for transfers between devices, per_device(): lax.ppermute(sketch, 'row', [(i, (i + 1) % halves) for i in range(halves)])  1.19 us
  transfers between devices with their start and end apart: 1, of which 1 were waited for; matrix products, arithmetic and copies ran while one was open for 0% of the time, Pallas kernels for 0%

profile of v1, /device:TPU:0, one launch (start us, length us, event | category | flops | bytes accessed | tf_op | source)
XLA Modules:
  0.0 31.3 jit_solution(15714702933225502263)
XLA Ops:
  0.0 2.7 %partial_sketch.1 = bf16[8,128,128]{2,1,0:T(8,128)(2,1)} custom-call(bf16[128,2048]{1,0:T(8,128)(2,1)} %theta_ref.1, s32[1,2048]{1,0:T(1,128)} %bitcast.7, s32[1,1024]{1,0:T(1,128)} %bitcast.8), custom_call_target="tpu_custom_call" | custom-call | tf_op jit(solution)/shard_map/partial_sketch/pallas_call | solution.py:46
  2.7 16.2 %all_to_all.10 = bf16[8,128,128]{2,1,0:T(8,128)(2,1)S(1)} all-to-all(bf16[8,128,128]{2,1,0:T(8,128)(2,1)} %partial_sketch.1), channel_id=1, replica_groups=mesh['real'=2,'col'=8,'row'=2] {'col'}, dimensions={0} | all-to-all | bytes 524288 | tf_op jit(solution)/shard_map/all_to_all | solution.py:61
  18.9 0.1 collective-permute-start
  19.0 1.2 %collective-permute-done = bf16[128,128]{1,0:T(8,128)(2,1)S(1)} collective-permute-done((bf16[128,128]{1,0:T(8,128)(2,1)S(1)}, bf16[128,128]{1,0:T(8,128)(2,1)S(1)}, u32[]{:S(2)}, u32[]{:S(2)}) %collective-permute-start) | collective-permute-done | bytes 32800 | tf_op jit(solution)/shard_map/ppermute | solution.py:63
  20.2 0.2 convolution_convert_fusion
  20.4 10.3 %all_to_all.11 = bf16[8,16,256]{2,1,0:T(8,128)(2,1)S(1)} all-to-all(bf16[8,16,256]{2,1,0:T(8,128)(2,1)S(1)} %bitcast.6), channel_id=1, replica_groups=mesh['real'=2,'col'=8,'row'=2] {'col'}, dimensions={0} | all-to-all | bytes 131072 | tf_op jit(solution)/shard_map/all_to_all | solution.py:67
  30.7 0.6 %multiply_bitcast_fusion = f32[1,1,16,256]{3,2,1,0:T(8,128)} fusion(f32[16,256]{1,0:T(8,128)S(1)} %convert_reduce_fusion.1), kind=kLoop, calls=%fused_computation.9 | loop fusion | flops 4096 | bytes 32768 | tf_op jit(solution)/shard_map/div | solution.py:68
  (4 shorter events, 0.1 us)
Async XLA Ops:
  18.9 1.3 %collective-permute-start = (bf16[128,128]{1,0:T(8,128)(2,1)S(1)}, bf16[128,128]{1,0:T(8,128)(2,1)S(1)}, u32[]{:S(2)}, u32[]{:S(2)}) collective-permute-start(bf16[128,128]{1,0:T(8,128)(2,1)S(1)} %multiply_convert_fusion), channel_id=1, source_target_pairs={{0,1},{1,0},{2,3},{3,2},{4,5},{5,4},{6,7},{7,6},{8,9},{9,8},{10,11... | collective-permute-start | bytes 98312 | tf_op jit(solution)/shard_map/ppermute | solution.py:63

commit v2 on v1

v2 whole, which is shorter than its diff:
```python
import functools

import jax
import jax.numpy as jnp
from jax import lax
from jax.experimental import pallas as pl
from jax.experimental.pallas import tpu as pltpu
from jax.sharding import PartitionSpec as P

SIDE = 128
STRIPS = 4


def sign_of(bits, shift=4):
    while shift:
        bits = bits ^ bits >> shift
        shift //= 2
    return (1 - 2 * (bits & 1)).astype(jnp.float32).astype(jnp.bfloat16)


def partial_kernel(theta_hbm, signs_hbm, kept_hbm, out_ref, theta_ref, signs_ref, kept_ref, table_ref, sems, *, by_block):
    copies = [
        pltpu.make_async_copy(source, target, sems.at[i])
        for i, (source, target) in enumerate(((kept_hbm, kept_ref), (signs_hbm, signs_ref), (theta_hbm, theta_ref)))
    ]
    for copy in copies:
        copy.start()
    rows, local = theta_ref.shape
    keep = kept_ref.shape[1]
    groups = local // SIDE
    first = lax.axis_index("col") * groups
    strip = keep // STRIPS

    def build(s):
        kept = kept_ref[:, s * strip : (s + 1) * strip]
        low = sign_of(lax.broadcasted_iota(jnp.int32, (SIDE, strip), 0) & kept)
        high = sign_of((first + lax.broadcasted_iota(jnp.int32, (groups, strip), 0)) & (kept >> 7))
        for group in range(groups):
            table_ref[group * SIDE : (group + 1) * SIDE, s * strip : (s + 1) * strip] = low * high[group : group + 1]

    copies[0].wait()
    build(0)
    copies[1].wait()
    copies[2].wait()
    theta_ref[...] = theta_ref[...] * signs_ref[...].astype(jnp.float32).astype(jnp.bfloat16)
    for s in range(STRIPS):
        if s + 1 < STRIPS:
            build(s + 1)
        part = jnp.dot(theta_ref[...], table_ref[:, s * strip : (s + 1) * strip], preferred_element_type=jnp.float32)
        if by_block:
            width = out_ref.shape[2]
            for block in range(strip // width):
                out_ref[s * (strip // width) + block] = part[:, block * width : (block + 1) * width].astype(jnp.bfloat16)
        else:
            out_ref[s * strip : (s + 1) * strip, :] = part.T.astype(jnp.bfloat16)


def partial_sketch(theta, signs, kept, parts):
    rows, local = theta.shape
    keep = kept.shape[0]
    width = keep // parts
    by_block = width % SIDE == 0
    shape = (parts, rows, width) if by_block else (keep, rows)
    inputs = (theta, signs.reshape(1, local), kept.reshape(1, keep))
    out = pl.pallas_call(
        functools.partial(partial_kernel, by_block=by_block),
        out_shape=pltpu.VMEM(shape, jnp.bfloat16),
        in_specs=[pl.BlockSpec(memory_space=pltpu.HBM)] * 3,
        out_specs=pl.BlockSpec(memory_space=pltpu.VMEM),
        scratch_shapes=[
            pltpu.VMEM((rows, local), jnp.bfloat16),
            pltpu.VMEM((1, local), jnp.int32),
            pltpu.VMEM((1, keep), jnp.int32),
            pltpu.VMEM((local, keep), jnp.bfloat16),
            pltpu.SemaphoreType.DMA((3,)),
        ],
        compiler_params=pltpu.CompilerParams(vmem_limit_bytes=32 << 20),
        name="partial_sketch",
    )(*(pltpu.with_memory_space_constraint(x, pltpu.HBM) for x in inputs))
    return out if by_block else out.reshape(parts, width, rows).swapaxes(1, 2)


def per_device(parts, halves, theta, signs, kept):
    keep = kept.shape[0]
    rows = theta.shape[0]
    part = partial_sketch(theta, signs, kept, parts)
    met = lax.all_to_all(part, "col", split_axis=0, concat_axis=0, tiled=True)
    sketch = (met.astype(jnp.float32).sum(0) / SIDE).astype(jnp.bfloat16)
    other = lax.ppermute(sketch, "row", [(i, (i + 1) % halves) for i in range(halves)])
    own = lax.axis_index("row") == 0
    both = jnp.concatenate([jnp.where(own, sketch, other), jnp.where(own, other, sketch)], axis=0)
    gram = jnp.dot(sketch, both.T, preferred_element_type=jnp.float32).astype(jnp.bfloat16)
    met = lax.all_to_all(gram.reshape(parts, rows // parts, -1), "col", split_axis=0, concat_axis=0, tiled=True)
    return (met.astype(jnp.float32).sum(0) / keep)[None, None]


def solution(mesh):
    return jax.shard_map(
        functools.partial(per_device, mesh.shape["col"], mesh.shape["row"]),
        mesh=mesh,
        in_specs=(P(("real", "row"), "col"), P(("real", "col")), P()),
        out_specs=P(("real", "row"), "col", None, None),
        check_vma=False,
    )
```

time: 31.5 us -> 30.6 us (0.971)
  Pallas kernels: 2.66 us -> 1.93 us
    pallas_call x1, Pallas kernels: 2.66 us -> 1.93 us  [partial_sketch(): pl.pallas_call(functools.partial(partial_kernel, by_block=by_block), out_...]
where the time goes in v2:
time: 30.6 us; the launch traced here: 30.4 us
  blocking collectives  26.3 us (86%)
  Pallas kernels  1.93 us (6%)
  waiting for transfers between devices  1.19 us (4%)
  other arithmetic  0.68 us (2%)
    all_to_all x1, blocking collectives, per_device(): met = lax.all_to_all(part, 'col', split_axis=0, concat_axis=0, tiled=True)  16 us
    all_to_all x1, blocking collectives, per_device(): lax.all_to_all(gram.reshape(parts, rows // parts, -1), 'col', split_axis=...  10.3 us
    pallas_call x1, Pallas kernels, partial_sketch(): pl.pallas_call(functools.partial(partial_kernel, by_block=by_block), out_...  1.93 us
    ppermute x1, waiting for transfers between devices, per_device(): lax.ppermute(sketch, 'row', [(i, (i + 1) % halves) for i in range(halves)])  1.19 us
  transfers between devices with their start and end apart: 1, of which 1 were waited for; matrix products, arithmetic and copies ran while one was open for 0% of the time, Pallas kernels for 0%

profile of v2, /device:TPU:0, one launch (start us, length us, event | category | flops | bytes accessed | tf_op | source)
XLA Modules:
  0.0 30.4 jit_solution(12235312776548180417)
XLA Ops:
  0.0 1.9 %partial_sketch.1 = bf16[8,128,128]{2,1,0:T(8,128)(2,1)S(1)} custom-call(bf16[128,2048]{1,0:T(8,128)(2,1)} %theta_hbm.1, s32[1,2048]{1,0:T(1,128)} %bitcast.7, s32[1,1024]{1,0:T(1,128)} %bitcast.8), custom_call_target="tpu_custom_call" | custom-call | tf_op jit(solution)/shard_map/partial_sketch/pallas_call | solution.py:65
  1.9 16.0 %all_to_all.10 = bf16[8,128,128]{2,1,0:T(8,128)(2,1)S(1)} all-to-all(bf16[8,128,128]{2,1,0:T(8,128)(2,1)S(1)} %partial_sketch.1), channel_id=1, replica_groups=mesh['real'=2,'col'=8,'row'=2] {'col'}, dimensions={0} | all-to-all | bytes 524288 | tf_op jit(solution)/shard_map/all_to_all | solution.py:87
  18.0 0.1 collective-permute-start
  18.1 1.2 %collective-permute-done = bf16[128,128]{1,0:T(8,128)(2,1)S(1)} collective-permute-done((bf16[128,128]{1,0:T(8,128)(2,1)S(1)}, bf16[128,128]{1,0:T(8,128)(2,1)S(1)}, u32[]{:S(2)}, u32[]{:S(2)}) %collective-permute-start) | collective-permute-done | bytes 32800 | tf_op jit(solution)/shard_map/ppermute | solution.py:89
  19.3 0.2 convolution_convert_fusion
  19.4 10.3 %all_to_all.11 = bf16[8,16,256]{2,1,0:T(8,128)(2,1)S(1)} all-to-all(bf16[8,16,256]{2,1,0:T(8,128)(2,1)S(1)} %bitcast.6), channel_id=1, replica_groups=mesh['real'=2,'col'=8,'row'=2] {'col'}, dimensions={0} | all-to-all | bytes 131072 | tf_op jit(solution)/shard_map/all_to_all | solution.py:93
  29.8 0.6 %multiply_bitcast_fusion = f32[1,1,16,256]{3,2,1,0:T(8,128)} fusion(f32[16,256]{1,0:T(8,128)S(1)} %convert_reduce_fusion.1), kind=kLoop, calls=%fused_computation.9 | loop fusion | flops 4096 | bytes 32768 | tf_op jit(solution)/shard_map/div | solution.py:94
  (4 shorter events, 0.1 us)
Async XLA Ops:
  18.0 1.3 %collective-permute-start = (bf16[128,128]{1,0:T(8,128)(2,1)S(1)}, bf16[128,128]{1,0:T(8,128)(2,1)S(1)}, u32[]{:S(2)}, u32[]{:S(2)}) collective-permute-start(bf16[128,128]{1,0:T(8,128)(2,1)S(1)} %multiply_convert_fusion), channel_id=1, source_target_pairs={{0,1},{1,0},{2,3},{3,2},{4,5},{5,4},{6,7},{7,6},{8,9},{9,8},{10,11... | collective-permute-start | bytes 98312 | tf_op jit(solution)/shard_map/ppermute | solution.py:89

commit v3 on v2

--- a/solution.py
+++ b/solution.py
@@ -18,7 +18,7 @@
     return (1 - 2 * (bits & 1)).astype(jnp.float32).astype(jnp.bfloat16)
 
 
-def partial_kernel(theta_hbm, signs_hbm, kept_hbm, out_ref, theta_ref, signs_ref, kept_ref, table_ref, sems, *, by_block):
+def partial_kernel(theta_hbm, signs_hbm, kept_hbm, out_ref, row_ref, theta_ref, signs_ref, kept_ref, table_ref, sems, *, by_block):
     copies = [
         pltpu.make_async_copy(source, target, sems.at[i])
         for i, (source, target) in enumerate(((kept_hbm, kept_ref), (signs_hbm, signs_ref), (theta_hbm, theta_ref)))
@@ -38,6 +38,7 @@
         for group in range(groups):
             table_ref[group * SIDE : (group + 1) * SIDE, s * strip : (s + 1) * strip] = low * high[group : group + 1]
 
+    row_ref[...] = jnp.full(row_ref.shape, lax.axis_index("row"), jnp.int32)
     copies[0].wait()
     build(0)
     copies[1].wait()
@@ -62,11 +63,11 @@
     by_block = width % SIDE == 0
     shape = (parts, rows, width) if by_block else (keep, rows)
     inputs = (theta, signs.reshape(1, local), kept.reshape(1, keep))
-    out = pl.pallas_call(
+    out, row = pl.pallas_call(
         functools.partial(partial_kernel, by_block=by_block),
-        out_shape=pltpu.VMEM(shape, jnp.bfloat16),
+        out_shape=(pltpu.VMEM(shape, jnp.bfloat16), pltpu.VMEM((1, width), jnp.int32)),
         in_specs=[pl.BlockSpec(memory_space=pltpu.HBM)] * 3,
-        out_specs=pl.BlockSpec(memory_space=pltpu.VMEM),
+        out_specs=(pl.BlockSpec(memory_space=pltpu.VMEM),) * 2,
         scratch_shapes=[
             pltpu.VMEM((rows, local), jnp.bfloat16),
             pltpu.VMEM((1, local), jnp.int32),
@@ -77,20 +78,27 @@
         compiler_params=pltpu.CompilerParams(vmem_limit_bytes=32 << 20),
         name="partial_sketch",
     )(*(pltpu.with_memory_space_constraint(x, pltpu.HBM) for x in inputs))
-    return out if by_block else out.reshape(parts, width, rows).swapaxes(1, 2)
+    return (out if by_block else out.reshape(parts, width, rows).swapaxes(1, 2)), row
+
+
+def exchange(blocks, order):
+    return lax.all_to_all(blocks, "col", split_axis=0, concat_axis=0, tiled=True, axis_index_groups=[order])
 
 
 def per_device(parts, halves, theta, signs, kept):
     keep = kept.shape[0]
     rows = theta.shape[0]
-    part = partial_sketch(theta, signs, kept, parts)
-    met = lax.all_to_all(part, "col", split_axis=0, concat_axis=0, tiled=True)
+    order = [(parts // 2 - i) % parts for i in range(parts)]
+    part, row = partial_sketch(theta, signs, kept, parts)
+    met, row = lax.optimization_barrier((exchange(part, order), row))
     sketch = (met.astype(jnp.float32).sum(0) / SIDE).astype(jnp.bfloat16)
     other = lax.ppermute(sketch, "row", [(i, (i + 1) % halves) for i in range(halves)])
-    own = lax.axis_index("row") == 0
+    own = row == 0
     both = jnp.concatenate([jnp.where(own, sketch, other), jnp.where(own, other, sketch)], axis=0)
-    gram = jnp.dot(sketch, both.T, preferred_element_type=jnp.float32).astype(jnp.bfloat16)
-    met = lax.all_to_all(gram.reshape(parts, rows // parts, -1), "col", split_axis=0, concat_axis=0, tiled=True)
+    blocks = sketch.reshape(parts, rows // parts, -1)
+    ordered = jnp.concatenate([blocks[i] for i in order], axis=0)
+    gram = jnp.dot(ordered, both.T, preferred_element_type=jnp.float32).astype(jnp.bfloat16)
+    met = exchange(gram.reshape(parts, rows // parts, -1), order)
     return (met.astype(jnp.float32).sum(0) / keep)[None, None]
 
 

time: 30.6 us -> 27.6 us (0.902)
  blocking collectives: 26.3 us -> 23.3 us
    all_to_all x2, blocking collectives: 26.3 us -> 23.3 us  [exchange(): lax.all_to_all(blocks, 'col', split_axis=0, concat_axis=0, tiled=True, ax...]
where the time goes in v3:
time: 27.6 us; the launch traced here: 27.4 us
  blocking collectives  23.3 us (84%)
  Pallas kernels  1.93 us (7%)
  waiting for transfers between devices  1.1 us (4%)
  other arithmetic  0.68 us (2%)
    all_to_all x2, blocking collectives, exchange(): lax.all_to_all(blocks, 'col', split_axis=0, concat_axis=0, tiled=True, ax...  23.3 us
    pallas_call x1, Pallas kernels, partial_sketch(): pl.pallas_call(functools.partial(partial_kernel, by_block=by_block), out_...  1.93 us
    ppermute x1, waiting for transfers between devices, per_device(): lax.ppermute(sketch, 'row', [(i, (i + 1) % halves) for i in range(halves)])  1.1 us
    div x1, other arithmetic, per_device(): return (met.astype(jnp.float32).sum(0) / keep)[None, None]  0.61 us
  transfers between devices with their start and end apart: 1, of which 1 were waited for; matrix products, arithmetic and copies ran while one was open for 0% of the time, Pallas kernels for 0%

profile of v3, /device:TPU:0, one launch (start us, length us, event | category | flops | bytes accessed | tf_op | source)
XLA Modules:
  0.0 27.4 jit_solution(14454824044326043906)
XLA Ops:
  0.0 1.9 %partial_sketch.1 = (bf16[8,128,128]{2,1,0:T(8,128)(2,1)S(1)}, s32[1,128]{1,0:T(1,128)S(1)}) custom-call(bf16[128,2048]{1,0:T(8,128)(2,1)} %theta_hbm.1, s32[1,2048]{1,0:T(1,128)} %bitcast.9, s32[1,1024]{1,0:T(1,128)} %bitcast.10), custom_call_target="tpu_custom_call" | custom-call | tf_op jit(solution)/shard_map/partial_sketch/pallas_call | solution.py:66
  1.9 14.7 %all_to_all.10 = bf16[8,128,128]{2,1,0:T(8,128)(2,1)S(1)} all-to-all(bf16[8,128,128]{2,1,0:T(8,128)(2,1)S(1)} %get-tuple-element.9), channel_id=1, replica_groups={{8,6,4,2,0,14,12,10},{9,7,5,3,1,15,13,11},{24,22,20,18,16,30,28,26},{25..., dimensions={0} | all-to-all | bytes 524288 | tf_op jit(solution)/shard_map/all_to_all | solution.py:85
  16.7 0.1 collective-permute-start
  16.9 1.1 %collective-permute-done = bf16[128,128]{1,0:T(8,128)(2,1)S(1)} collective-permute-done((bf16[128,128]{1,0:T(8,128)(2,1)S(1)}, bf16[128,128]{1,0:T(8,128)(2,1)S(1)}, u32[]{:S(2)}, u32[]{:S(2)}) %collective-permute-start) | collective-permute-done | bytes 32800 | tf_op jit(solution)/shard_map/ppermute | solution.py:95
  18.0 0.2 convolution_convert_fusion
  18.2 8.6 %all_to_all.11 = bf16[8,16,256]{2,1,0:T(8,128)(2,1)S(1)} all-to-all(bf16[8,16,256]{2,1,0:T(8,128)(2,1)S(1)} %bitcast.8), channel_id=1, replica_groups={{8,6,4,2,0,14,12,10},{9,7,5,3,1,15,13,11},{24,22,20,18,16,30,28,26},{25..., dimensions={0} | all-to-all | bytes 131072 | tf_op jit(solution)/shard_map/all_to_all | solution.py:85
  26.8 0.6 %multiply_bitcast_fusion = f32[1,1,16,256]{3,2,1,0:T(8,128)} fusion(f32[16,256]{1,0:T(8,128)S(1)} %convert_reduce_fusion.1), kind=kLoop, calls=%fused_computation.17 | loop fusion | flops 4096 | bytes 32768 | tf_op jit(solution)/shard_map/div | solution.py:102
  (13 shorter events, 0.1 us)
Async XLA Ops:
  16.7 1.3 %collective-permute-start = (bf16[128,128]{1,0:T(8,128)(2,1)S(1)}, bf16[128,128]{1,0:T(8,128)(2,1)S(1)}, u32[]{:S(2)}, u32[]{:S(2)}) collective-permute-start(bf16[128,128]{1,0:T(8,128)(2,1)S(1)} %multiply_convert_fusion), channel_id=1, source_target_pairs={{0,1},{1,0},{2,3},{3,2},{4,5},{5,4},{6,7},{7,6},{8,9},{9,8},{10,11... | collective-permute-start | bytes 98312 | tf_op jit(solution)/shard_map/ppermute | solution.py:95

commit v4 on v3

--- a/solution.py
+++ b/solution.py
@@ -88,7 +88,7 @@
 def per_device(parts, halves, theta, signs, kept):
     keep = kept.shape[0]
     rows = theta.shape[0]
-    order = [(parts // 2 - i) % parts for i in range(parts)]
+    order = [(parts // 2 + 1 + 3 * i) % parts for i in range(parts)]
     part, row = partial_sketch(theta, signs, kept, parts)
     met, row = lax.optimization_barrier((exchange(part, order), row))
     sketch = (met.astype(jnp.float32).sum(0) / SIDE).astype(jnp.bfloat16)

time: 27.6 us -> 26.8 us (0.971)
  blocking collectives: 23.3 us -> 22.5 us
    all_to_all x2, blocking collectives: 23.3 us -> 22.5 us  [exchange(): lax.all_to_all(blocks, 'col', split_axis=0, concat_axis=0, tiled=True, ax...]
where the time goes in v4:
time: 26.8 us; the launch traced here: 26.6 us
  blocking collectives  22.5 us (84%)
  Pallas kernels  1.93 us (7%)
  waiting for transfers between devices  1.1 us (4%)
  other arithmetic  0.68 us (3%)
    all_to_all x2, blocking collectives, exchange(): lax.all_to_all(blocks, 'col', split_axis=0, concat_axis=0, tiled=True, ax...  22.5 us
    pallas_call x1, Pallas kernels, partial_sketch(): pl.pallas_call(functools.partial(partial_kernel, by_block=by_block), out_...  1.93 us
    ppermute x1, waiting for transfers between devices, per_device(): lax.ppermute(sketch, 'row', [(i, (i + 1) % halves) for i in range(halves)])  1.1 us
    div x1, other arithmetic, per_device(): return (met.astype(jnp.float32).sum(0) / keep)[None, None]  0.61 us
  transfers between devices with their start and end apart: 1, of which 1 were waited for; matrix products, arithmetic and copies ran while one was open for 0% of the time, Pallas kernels for 0%

profile of v4, /device:TPU:0, one launch (start us, length us, event | category | flops | bytes accessed | tf_op | source)
XLA Modules:
  0.0 26.6 jit_solution(15309050508033812219)
XLA Ops:
  0.0 1.9 %partial_sketch.1 = (bf16[8,128,128]{2,1,0:T(8,128)(2,1)S(1)}, s32[1,128]{1,0:T(1,128)S(1)}) custom-call(bf16[128,2048]{1,0:T(8,128)(2,1)} %theta_hbm.1, s32[1,2048]{1,0:T(1,128)} %bitcast.9, s32[1,1024]{1,0:T(1,128)} %bitcast.10), custom_call_target="tpu_custom_call" | custom-call | tf_op jit(solution)/shard_map/partial_sketch/pallas_call | solution.py:66
  1.9 14.2 %all_to_all.10 = bf16[8,128,128]{2,1,0:T(8,128)(2,1)S(1)} all-to-all(bf16[8,128,128]{2,1,0:T(8,128)(2,1)S(1)} %get-tuple-element.9), channel_id=1, replica_groups={{10,0,6,12,2,8,14,4},{11,1,7,13,3,9,15,5},{26,16,22,28,18,24,30,20},{27..., dimensions={0} | all-to-all | bytes 524288 | tf_op jit(solution)/shard_map/all_to_all | solution.py:85
  16.2 0.1 collective-permute-start
  16.4 1.1 %collective-permute-done = bf16[128,128]{1,0:T(8,128)(2,1)S(1)} collective-permute-done((bf16[128,128]{1,0:T(8,128)(2,1)S(1)}, bf16[128,128]{1,0:T(8,128)(2,1)S(1)}, u32[]{:S(2)}, u32[]{:S(2)}) %collective-permute-start) | collective-permute-done | bytes 32800 | tf_op jit(solution)/shard_map/ppermute | solution.py:95
  17.5 0.2 convolution_convert_fusion
  17.6 8.3 %all_to_all.11 = bf16[8,16,256]{2,1,0:T(8,128)(2,1)S(1)} all-to-all(bf16[8,16,256]{2,1,0:T(8,128)(2,1)S(1)} %bitcast.8), channel_id=1, replica_groups={{10,0,6,12,2,8,14,4},{11,1,7,13,3,9,15,5},{26,16,22,28,18,24,30,20},{27..., dimensions={0} | all-to-all | bytes 131072 | tf_op jit(solution)/shard_map/all_to_all | solution.py:85
  25.9 0.6 %multiply_bitcast_fusion = f32[1,1,16,256]{3,2,1,0:T(8,128)} fusion(f32[16,256]{1,0:T(8,128)S(1)} %convert_reduce_fusion.1), kind=kLoop, calls=%fused_computation.17 | loop fusion | flops 4096 | bytes 32768 | tf_op jit(solution)/shard_map/div | solution.py:102
  (13 shorter events, 0.1 us)
Async XLA Ops:
  16.2 1.3 %collective-permute-start = (bf16[128,128]{1,0:T(8,128)(2,1)S(1)}, bf16[128,128]{1,0:T(8,128)(2,1)S(1)}, u32[]{:S(2)}, u32[]{:S(2)}) collective-permute-start(bf16[128,128]{1,0:T(8,128)(2,1)S(1)} %multiply_convert_fusion), channel_id=1, source_target_pairs={{0,1},{1,0},{2,3},{3,2},{4,5},{5,4},{6,7},{7,6},{8,9},{9,8},{10,11... | collective-permute-start | bytes 98312 | tf_op jit(solution)/shard_map/ppermute | solution.py:95

commit v5 on v2

v5 whole, which is shorter than its diff:
```python
import functools

import jax
import jax.numpy as jnp
from jax import lax
from jax.experimental import pallas as pl
from jax.experimental.pallas import tpu as pltpu
from jax.sharding import PartitionSpec as P

SIDE = 128
STRIPS = 4
TILE = 16


def sign_of(bits, shift=4):
    while shift:
        bits = bits ^ bits >> shift
        shift //= 2
    return (1 - 2 * (bits & 1)).astype(jnp.float32).astype(jnp.bfloat16)


def partial_kernel(theta_hbm, signs_hbm, kept_hbm, out_ref, theta_ref, signs_ref, kept_ref, table_ref, sems):
    copies = [
        pltpu.make_async_copy(source, target, sems.at[i])
        for i, (source, target) in enumerate(((theta_hbm, theta_ref), (kept_hbm, kept_ref), (signs_hbm, signs_ref)))
    ]
    for copy in copies:
        copy.start()
    local = theta_ref.shape[1]
    keep = kept_ref.shape[1]
    groups = local // SIDE
    first = lax.axis_index("col") * groups
    strip = keep // STRIPS

    def sign_rows(count, bits):
        return sign_of(lax.broadcasted_iota(jnp.int32, (count, strip), 0) & bits)

    def build(s):
        kept = kept_ref[:, s * strip : (s + 1) * strip]
        low, middle = sign_rows(TILE, kept & (TILE - 1)), sign_rows(SIDE // TILE, kept // TILE & (SIDE // TILE - 1))
        inner = jnp.concatenate([low * middle[i : i + 1] for i in range(SIDE // TILE)], axis=0)
        high = sign_of((first + lax.broadcasted_iota(jnp.int32, (groups, strip), 0)) & (kept >> 7))
        for group in range(groups):
            table_ref[group * SIDE : (group + 1) * SIDE, s * strip : (s + 1) * strip] = inner * high[group : group + 1]

    copies[1].wait()
    build(0)
    build(1)
    copies[2].wait()
    copies[0].wait()
    theta_ref[...] = theta_ref[...] * signs_ref[...].astype(jnp.float32).astype(jnp.bfloat16)
    for s in range(STRIPS):
        if s + 2 < STRIPS:
            build(s + 2)
        part = jnp.dot(theta_ref[...], table_ref[:, s * strip : (s + 1) * strip], preferred_element_type=jnp.float32)
        out_ref[s * strip : (s + 1) * strip, :] = part.T.astype(jnp.bfloat16)


def partial_sketch(theta, signs, kept):
    rows, local = theta.shape
    keep = kept.shape[0]
    inputs = (theta, signs.reshape(1, local), kept.reshape(1, keep))
    return pl.pallas_call(
        partial_kernel,
        out_shape=pltpu.VMEM((keep, rows), jnp.bfloat16),
        in_specs=[pl.BlockSpec(memory_space=pltpu.HBM)] * 3,
        out_specs=pl.BlockSpec(memory_space=pltpu.VMEM),
        scratch_shapes=[
            pltpu.VMEM((rows, local), jnp.bfloat16),
            pltpu.VMEM((1, local), jnp.int32),
            pltpu.VMEM((1, keep), jnp.int32),
            pltpu.VMEM((local, keep), jnp.bfloat16),
            pltpu.SemaphoreType.DMA((3,)),
        ],
        compiler_params=pltpu.CompilerParams(vmem_limit_bytes=32 << 20),
        name="partial_sketch",
    )(*(pltpu.with_memory_space_constraint(x, pltpu.HBM) for x in inputs))


def gram_kernel(met_ref, out_ref, *, rows_of, targets, halves):
    sums = [
        sum(met_ref[i].astype(jnp.float32) for i, row in enumerate(rows_of) if row == half) * (1 / SIDE)
        for half in range(halves)
    ]
    columns = jnp.concatenate([total.astype(jnp.bfloat16) for total in sums], axis=1)
    grams = [
        jnp.dot(total.T.astype(jnp.bfloat16), columns, preferred_element_type=jnp.float32).astype(jnp.bfloat16)
        for total in sums
    ]
    block = out_ref.shape[1]
    for i, (col, row) in enumerate(targets):
        out_ref[i] = grams[row][col * block : (col + 1) * block]


def partial_gram(met, rows_of, targets, parts, rows, halves):
    return pl.pallas_call(
        functools.partial(gram_kernel, rows_of=rows_of, targets=targets, halves=halves),
        out_shape=pltpu.VMEM((len(targets), rows // parts, halves * rows), jnp.bfloat16),
        in_specs=[pl.BlockSpec(memory_space=pltpu.VMEM)],
        out_specs=pl.BlockSpec(memory_space=pltpu.VMEM),
        compiler_params=pltpu.CompilerParams(vmem_limit_bytes=16 << 20),
        name="partial_gram",
    )(met)


def exchange(blocks, axes, order):
    return lax.all_to_all(blocks, axes, split_axis=0, concat_axis=0, tiled=True, axis_index_groups=[order])


def by_pair(part, parts, halves):
    rows = part.shape[1]
    size = parts * halves
    leader = (parts // 2 + 2) * halves - 1
    first, second = ([(leader + step * i) % size for i in range(size)] for step in (7, 5))
    met = exchange(part.reshape(size, -1, rows), ("col", "row"), first)
    rows_of = [i % halves for i in first]
    targets = [(i // halves, i % halves) for i in second]
    return exchange(partial_gram(met, rows_of, targets, parts, rows, halves), ("col", "row"), second)


def by_column(part, parts, halves):
    rows = part.shape[1]
    order = [(parts // 2 + 1 + 3 * i) % parts for i in range(parts)]
    met = exchange(part.reshape(parts, -1, rows), "col", order)
    sketch = (met.astype(jnp.float32).sum(0) / SIDE).astype(jnp.bfloat16)
    both = lax.all_gather(sketch, "row", axis=1, tiled=True)
    gram = lax.dot_general(sketch, both, (((0,), (0,)), ((), ())), preferred_element_type=jnp.float32)
    blocks = gram.astype(jnp.bfloat16).reshape(parts, rows // parts, -1)
    return exchange(jnp.concatenate([blocks[i : i + 1] for i in order]), "col", order)


def per_device(parts, halves, theta, signs, kept):
    keep = kept.shape[0]
    part = partial_sketch(theta, signs, kept)
    whole_tiles = keep % (parts * halves * TILE) == 0
    met = (by_pair if whole_tiles else by_column)(part, parts, halves)
    return (met.astype(jnp.float32).sum(0) / keep)[None, None]


def solution(mesh):
    return jax.shard_map(
        functools.partial(per_device, mesh.shape["col"], mesh.shape["row"]),
        mesh=mesh,
        in_specs=(P(("real", "row"), "col"), P(("real", "col")), P()),
        out_specs=P(("real", "row"), "col", None, None),
        check_vma=False,
    )
```

time: 30.6 us -> 25.8 us (0.84)
  blocking collectives: 26.3 us -> 22.7 us
  waiting for transfers between devices: 1.19 us -> 0 us
    all_to_all x2, blocking collectives: 26.3 us -> 22.7 us  [exchange(): lax.all_to_all(blocks, axes, split_axis=0, concat_axis=0, tiled=True, axi...]
    ppermute x1 -> x0, waiting for transfers between devices: 1.19 us -> none  [per_device(): lax.ppermute(sketch, 'row', [(i, (i + 1) % halves) for i in range(halves)])]
    pallas_call x1 -> x2, Pallas kernels: 1.93 us -> 2.12 us  [the longest x1 1.88 us: partial_sketch(): pl.pallas_call(partial_kernel, out_shape=pltpu.VMEM((keep, rows), jnp.bfl...]
  transfers between devices with their start and end apart: 1 -> 0, of which waited for: 1 -> 0; matrix products, arithmetic and copies ran while one was open for 0% -> 0% of each run, Pallas kernels for 0% -> 0%
where the time goes in v5:
time: 25.8 us; the launch traced here: 25.5 us
  blocking collectives  22.7 us (88%)
  Pallas kernels  2.12 us (8%)
  other arithmetic  0.63 us (2%)
    all_to_all x2, blocking collectives, exchange(): lax.all_to_all(blocks, axes, split_axis=0, concat_axis=0, tiled=True, axi...  22.7 us
    pallas_call x1, Pallas kernels, partial_sketch(): pl.pallas_call(partial_kernel, out_shape=pltpu.VMEM((keep, rows), jnp.bfl...  1.88 us
    div x1, other arithmetic, per_device(): return (met.astype(jnp.float32).sum(0) / keep)[None, None]  0.61 us

profile of v5, /device:TPU:0, one launch (start us, length us, event | category | flops | bytes accessed | tf_op | source)
XLA Modules:
  0.0 25.5 jit_solution(10338780999364095018)
XLA Ops:
  0.0 1.9 %partial_sketch.1 = bf16[1024,128]{1,0:T(8,128)(2,1)S(1)} custom-call(bf16[128,2048]{1,0:T(8,128)(2,1)} %theta_hbm.1, s32[1,2048]{1,0:T(1,128)} %bitcast.6, s32[1,1024]{1,0:T(1,128)} %bitcast.7), custom_call_target="tpu_custom_call" | custom-call | tf_op jit(solution)/shard_map/partial_sketch/pallas_call | solution.py:63
  1.9 13.3 %all_to_all.10.met_ref = bf16[16,64,128]{2,1,0:T(8,128)(2,1)S(1)} all-to-all(bf16[16,64,128]{2,1,0:T(8,128)(2,1)S(1)} %bitcast.5), channel_id=1, replica_groups={{11,2,9,0,7,14,5,12,3,10,1,8,15,6,13,4},{27,18,25,16,23,30,21,28,19,26,..., dimensions={0} | all-to-all | bytes 524288 | tf_op jit(solution)/shard_map/all_to_all | solution.py:107
  15.2 0.2 partial_gram.1
  15.5 9.4 %all_to_all.11 = bf16[16,16,256]{2,1,0:T(8,128)(2,1)S(1)} all-to-all(bf16[16,16,256]{2,1,0:T(8,128)(2,1)S(1)} %partial_gram.1), channel_id=1, replica_groups={{11,0,5,10,15,4,9,14,3,8,13,2,7,12,1,6},{27,16,21,26,31,20,25,30,19,24,..., dimensions={0} | all-to-all | bytes 262144 | tf_op jit(solution)/shard_map/all_to_all | solution.py:107
  24.9 0.6 %multiply_bitcast_fusion = f32[1,1,16,256]{3,2,1,0:T(8,128)} fusion(f32[16,256]{1,0:T(8,128)S(1)} %convert_reduce_fusion), kind=kLoop, calls=%fused_computation.1 | loop fusion | flops 4096 | bytes 32768 | tf_op jit(solution)/shard_map/div | solution.py:137
  (1 shorter events, 0.0 us)

commit v6 on v5

--- a/solution.py
+++ b/solution.py
@@ -111,7 +111,8 @@
     rows = part.shape[1]
     size = parts * halves
     leader = (parts // 2 + 2) * halves - 1
-    first, second = ([(leader + step * i) % size for i in range(size)] for step in (7, 5))
+    first = [leader ^ i for i in range(size)]
+    second = [(leader + 5 * i) % size for i in range(size)]
     met = exchange(part.reshape(size, -1, rows), ("col", "row"), first)
     rows_of = [i % halves for i in first]
     targets = [(i // halves, i % halves) for i in second]

time: 25.8 us -> 25.7 us (level)
  no operation moved by 1% of the time
where the time goes in v6:
time: 25.7 us; the launch traced here: 25.4 us
  blocking collectives  22.6 us (88%)
  Pallas kernels  2.12 us (8%)
  other arithmetic  0.63 us (2%)
    all_to_all x2, blocking collectives, exchange(): lax.all_to_all(blocks, axes, split_axis=0, concat_axis=0, tiled=True, axi...  22.6 us
    pallas_call x1, Pallas kernels, partial_sketch(): pl.pallas_call(partial_kernel, out_shape=pltpu.VMEM((keep, rows), jnp.bfl...  1.88 us
    div x1, other arithmetic, per_device(): return (met.astype(jnp.float32).sum(0) / keep)[None, None]  0.61 us

profile of v6, /device:TPU:0, one launch (start us, length us, event | category | flops | bytes accessed | tf_op | source)
XLA Modules:
  0.0 25.4 jit_solution(1986824057398670293)
XLA Ops:
  0.0 1.9 %partial_sketch.1 = bf16[1024,128]{1,0:T(8,128)(2,1)S(1)} custom-call(bf16[128,2048]{1,0:T(8,128)(2,1)} %theta_hbm.1, s32[1,2048]{1,0:T(1,128)} %bitcast.6, s32[1,1024]{1,0:T(1,128)} %bitcast.7), custom_call_target="tpu_custom_call" | custom-call | tf_op jit(solution)/shard_map/partial_sketch/pallas_call | solution.py:63
  1.9 12.3 %all_to_all.10.met_ref = bf16[16,64,128]{2,1,0:T(8,128)(2,1)S(1)} all-to-all(bf16[16,64,128]{2,1,0:T(8,128)(2,1)S(1)} %bitcast.5), channel_id=1, replica_groups={{11,10,9,8,15,14,13,12,3,2,1,0,7,6,5,4},{27,26,25,24,31,30,29,28,19,18,..., dimensions={0} | all-to-all | bytes 524288 | tf_op jit(solution)/shard_map/all_to_all | solution.py:107
  14.2 0.2 partial_gram.1
  14.4 10.4 %all_to_all.11 = bf16[16,16,256]{2,1,0:T(8,128)(2,1)S(1)} all-to-all(bf16[16,16,256]{2,1,0:T(8,128)(2,1)S(1)} %partial_gram.1), channel_id=1, replica_groups={{11,0,5,10,15,4,9,14,3,8,13,2,7,12,1,6},{27,16,21,26,31,20,25,30,19,24,..., dimensions={0} | all-to-all | bytes 262144 | tf_op jit(solution)/shard_map/all_to_all | solution.py:107
  24.8 0.6 %multiply_bitcast_fusion = f32[1,1,16,256]{3,2,1,0:T(8,128)} fusion(f32[16,256]{1,0:T(8,128)S(1)} %convert_reduce_fusion), kind=kLoop, calls=%fused_computation.1 | loop fusion | flops 4096 | bytes 32768 | tf_op jit(solution)/shard_map/div | solution.py:138
  (1 shorter events, 0.0 us)

commit v7 on v5

--- a/solution.py
+++ b/solution.py
@@ -107,11 +107,16 @@
     return lax.all_to_all(blocks, axes, split_axis=0, concat_axis=0, tiled=True, axis_index_groups=[order])
 
 
+def member_order(size, leader, step, runs):
+    cut = size // runs
+    return [(leader + step * (i % cut * runs + i // cut)) % size for i in range(size)]
+
+
 def by_pair(part, parts, halves):
     rows = part.shape[1]
     size = parts * halves
     leader = (parts // 2 + 2) * halves - 1
-    first, second = ([(leader + step * i) % size for i in range(size)] for step in (7, 5))
+    first, second = member_order(size, leader, 7, 4), member_order(size, leader, 9, 8)
     met = exchange(part.reshape(size, -1, rows), ("col", "row"), first)
     rows_of = [i % halves for i in first]
     targets = [(i // halves, i % halves) for i in second]

time: 25.8 us -> 25.4 us (0.984)
  blocking collectives: 22.7 us -> 22.3 us
    all_to_all x2, blocking collectives: 22.7 us -> 22.3 us  [exchange(): lax.all_to_all(blocks, axes, split_axis=0, concat_axis=0, tiled=True, axi...]
where the time goes in v7:
time: 25.4 us; the launch traced here: 25 us
  blocking collectives  22.3 us (88%)
  Pallas kernels  2.13 us (8%)
  other arithmetic  0.63 us (2%)
    all_to_all x2, blocking collectives, exchange(): lax.all_to_all(blocks, axes, split_axis=0, concat_axis=0, tiled=True, axi...  22.3 us
    pallas_call x1, Pallas kernels, partial_sketch(): pl.pallas_call(partial_kernel, out_shape=pltpu.VMEM((keep, rows), jnp.bfl...  1.88 us
    div x1, other arithmetic, per_device(): return (met.astype(jnp.float32).sum(0) / keep)[None, None]  0.61 us

profile of v7, /device:TPU:0, one launch (start us, length us, event | category | flops | bytes accessed | tf_op | source)
XLA Modules:
  0.0 25.0 jit_solution(14915436979158775669)
XLA Ops:
  0.0 1.9 %partial_sketch.1 = bf16[1024,128]{1,0:T(8,128)(2,1)S(1)} custom-call(bf16[128,2048]{1,0:T(8,128)(2,1)} %theta_hbm.1, s32[1,2048]{1,0:T(1,128)} %bitcast.6, s32[1,1024]{1,0:T(1,128)} %bitcast.7), custom_call_target="tpu_custom_call" | custom-call | tf_op jit(solution)/shard_map/partial_sketch/pallas_call | solution.py:63
  1.9 14.1 %all_to_all.10.met_ref = bf16[16,64,128]{2,1,0:T(8,128)(2,1)S(1)} all-to-all(bf16[16,64,128]{2,1,0:T(8,128)(2,1)S(1)} %bitcast.5), channel_id=1, replica_groups={{11,7,3,15,2,14,10,6,9,5,1,13,0,12,8,4},{27,23,19,31,18,30,26,22,25,21,..., dimensions={0} | all-to-all | bytes 524288 | tf_op jit(solution)/shard_map/all_to_all | solution.py:107
  16.0 0.2 partial_gram.1
  16.2 8.2 %all_to_all.11 = bf16[16,16,256]{2,1,0:T(8,128)(2,1)S(1)} all-to-all(bf16[16,16,256]{2,1,0:T(8,128)(2,1)S(1)} %partial_gram.1), channel_id=1, replica_groups={{11,3,4,12,13,5,6,14,15,7,8,0,1,9,10,2},{27,19,20,28,29,21,22,30,31,23,..., dimensions={0} | all-to-all | bytes 262144 | tf_op jit(solution)/shard_map/all_to_all | solution.py:107
  24.4 0.6 %multiply_bitcast_fusion = f32[1,1,16,256]{3,2,1,0:T(8,128)} fusion(f32[16,256]{1,0:T(8,128)S(1)} %convert_reduce_fusion), kind=kLoop, calls=%fused_computation.1 | loop fusion | flops 4096 | bytes 32768 | tf_op jit(solution)/shard_map/div | solution.py:142
  (1 shorter events, 0.0 us)

commit v8 on v7

--- a/solution.py
+++ b/solution.py
@@ -83,13 +83,13 @@
         for half in range(halves)
     ]
     columns = jnp.concatenate([total.astype(jnp.bfloat16) for total in sums], axis=1)
-    grams = [
-        jnp.dot(total.T.astype(jnp.bfloat16), columns, preferred_element_type=jnp.float32).astype(jnp.bfloat16)
-        for total in sums
-    ]
+    contract = (((0,), (0,)), ((), ()))
+    gram = lax.dot_general(columns, columns, contract, preferred_element_type=jnp.float32).astype(jnp.bfloat16)
+    rows = gram.shape[0] // halves
     block = out_ref.shape[1]
     for i, (col, row) in enumerate(targets):
-        out_ref[i] = grams[row][col * block : (col + 1) * block]
+        start = row * rows + col * block
+        out_ref[i] = gram[start : start + block]
 
 
 def partial_gram(met, rows_of, targets, parts, rows, halves):

time: 25.4 us -> 25.4 us (level)
  no operation moved by 1% of the time
where the time goes in v8:
time: 25.4 us; the launch traced here: 25 us
  blocking collectives  22.3 us (88%)
  Pallas kernels  2.11 us (8%)
  other arithmetic  0.63 us (2%)
    all_to_all x2, blocking collectives, exchange(): lax.all_to_all(blocks, axes, split_axis=0, concat_axis=0, tiled=True, axi...  22.3 us
    pallas_call x1, Pallas kernels, partial_sketch(): pl.pallas_call(partial_kernel, out_shape=pltpu.VMEM((keep, rows), jnp.bfl...  1.88 us
    div x1, other arithmetic, per_device(): return (met.astype(jnp.float32).sum(0) / keep)[None, None]  0.61 us

profile of v8, /device:TPU:0, one launch (start us, length us, event | category | flops | bytes accessed | tf_op | source)
XLA Modules:
  0.0 25.0 jit_solution(14510388400278825288)
XLA Ops:
  0.0 1.9 %partial_sketch.1 = bf16[1024,128]{1,0:T(8,128)(2,1)S(1)} custom-call(bf16[128,2048]{1,0:T(8,128)(2,1)} %theta_hbm.1, s32[1,2048]{1,0:T(1,128)} %bitcast.6, s32[1,1024]{1,0:T(1,128)} %bitcast.7), custom_call_target="tpu_custom_call" | custom-call | tf_op jit(solution)/shard_map/partial_sketch/pallas_call | solution.py:63
  1.9 14.1 %all_to_all.10.met_ref = bf16[16,64,128]{2,1,0:T(8,128)(2,1)S(1)} all-to-all(bf16[16,64,128]{2,1,0:T(8,128)(2,1)S(1)} %bitcast.5), channel_id=1, replica_groups={{11,7,3,15,2,14,10,6,9,5,1,13,0,12,8,4},{27,23,19,31,18,30,26,22,25,21,..., dimensions={0} | all-to-all | bytes 524288 | tf_op jit(solution)/shard_map/all_to_all | solution.py:107
  16.0 0.2 partial_gram.1
  16.2 8.2 %all_to_all.11 = bf16[16,16,256]{2,1,0:T(8,128)(2,1)S(1)} all-to-all(bf16[16,16,256]{2,1,0:T(8,128)(2,1)S(1)} %partial_gram.1), channel_id=1, replica_groups={{11,3,4,12,13,5,6,14,15,7,8,0,1,9,10,2},{27,19,20,28,29,21,22,30,31,23,..., dimensions={0} | all-to-all | bytes 262144 | tf_op jit(solution)/shard_map/all_to_all | solution.py:107
  24.4 0.6 %multiply_bitcast_fusion = f32[1,1,16,256]{3,2,1,0:T(8,128)} fusion(f32[16,256]{1,0:T(8,128)S(1)} %convert_reduce_fusion), kind=kLoop, calls=%fused_computation.1 | loop fusion | flops 4096 | bytes 32768 | tf_op jit(solution)/shard_map/div | solution.py:142
  (1 shorter events, 0.0 us)
